TPU v7x, 32 devices: a whole 2x2x4 slice. The times are simulated.
32 devices in a mesh: gx: 4 (over x, core), gy: 8 (over z, y).
Axes of the slice: x: 2, y: 2, z: 4, core: 2. Of those that a mesh axis runs over, the one named last changes fastest.
Arguments:
- populations: float32 [19, 32, 64, 128], P(None, 'gx', 'gy'), may hold values from 0 to 1, as said below
- cell_kind: int32 [32, 64, 128], P('gx', 'gy'), may hold values from 0 to 3, as said below
- outlet_region: int32 [32, 64], P('gx', 'gy'), may hold values from 0 to 63, as said below
Outputs:
- final_populations: float32 [19, 32, 64, 128], P(None, 'gx', 'gy')
- outlet_means: float32 [2, 64], replicated
Inputs may be any that keep to these rules, and one draw needn't show every extreme that they name: `populations`: positive. `cell_kind`: the plane z = 0 is all inlet (2), the plane z = 127 all outlet (3); all other cells are fluid (0) or wall (1). `outlet_region`: every region names at least one column; ids are constant on aligned tiles of 4 x 4 columns.
All inputs are finite; a program needn't handle non-finite values.
Results may differ from a plain program's by a relative error of at most 0.0001.
Values sent between devices are 32-bit elements; how exact they have to be, the bound alone decides.
A program may use at most 64 MiB of HBM per device.

v0:
```python
import jax
import jax.numpy as jnp
from jax import lax
from jax.sharding import PartitionSpec as P

REGIONS = 64
STEPS = 2
VELOCITIES = (
    (0, 0, 0),
    (1, 0, 0),
    (-1, 0, 0),
    (0, 1, 0),
    (0, -1, 0),
    (0, 0, 1),
    (0, 0, -1),
    (1, 1, 0),
    (-1, -1, 0),
    (1, -1, 0),
    (-1, 1, 0),
    (1, 0, 1),
    (-1, 0, -1),
    (1, 0, -1),
    (-1, 0, 1),
    (0, 1, 1),
    (0, -1, -1),
    (0, 1, -1),
    (0, -1, 1),
)
WEIGHTS = (1.0 / 3.0,) + (1.0 / 18.0,) * 6 + (1.0 / 36.0,) * 12
OPPOSITE = (0, 2, 1, 4, 3, 6, 5, 8, 7, 10, 9, 12, 11, 14, 13, 16, 15, 18, 17)
RELAX_TIME = 0.8
INLET_SPEED = 0.05
RISING_X = (1, 7, 9, 11, 13)
FALLING_X = (2, 8, 10, 12, 14)
RISING_Y = (3, 7, 10, 15, 17)
FALLING_Y = (4, 8, 9, 16, 18)


def from_behind(block, axis, distance):
    devices = range(lax.axis_size(axis))
    route = [(i - distance, i) for i in devices if i - distance in devices]
    return lax.ppermute(block, axis, route)


def from_behind_2(value, axis, steps):
    count = lax.axis_size(axis)
    pairs = [(source, (source + steps) % count) for source in range(count)]
    return lax.ppermute(value, axis, pairs)


def momentum(current, direction):
    total = jnp.zeros_like(current[0])
    for number in range(19):
        factor = VELOCITIES[number][direction]
        if factor != 0:
            total = total + factor * current[number]
    return total


def equilibrium(density, vel_x, vel_y, vel_z):
    speed_sq = vel_x * vel_x + vel_y * vel_y + vel_z * vel_z
    result = []
    for number in range(19):
        comp_x, comp_y, comp_z = VELOCITIES[number]
        projected = comp_x * vel_x + comp_y * vel_y + comp_z * vel_z
        result.append(
            WEIGHTS[number]
            * density
            * (1.0 + 3.0 * projected + 4.5 * projected * projected - 1.5 * speed_sq)
        )
    return jnp.stack(result)


def collide(current, kinds, col_mean):
    density = jnp.sum(current, axis=0)
    vel_x = momentum(current, 0) / density
    vel_y = momentum(current, 1) / density
    vel_z = momentum(current, 2) / density
    relaxed = current - (current - equilibrium(density, vel_x, vel_y, vel_z)) / RELAX_TIME
    bounced = jnp.stack([current[OPPOSITE[number]] for number in range(19)])
    unity = jnp.ones_like(density)
    still = jnp.zeros_like(density)
    inlet = equilibrium(unity, still, still, INLET_SPEED * unity)
    outlet = equilibrium(col_mean * unity, vel_x, vel_y, vel_z)
    post = jnp.where(kinds == 1, bounced, relaxed)
    post = jnp.where(kinds == 2, inlet, post)
    post = jnp.where(kinds == 3, outlet, post)
    return post


def stream(padded, rows_x, rows_y):
    moved = []
    for number in range(19):
        comp_x, comp_y, comp_z = VELOCITIES[number]
        plane = padded[
            number, 1 - comp_x : 1 - comp_x + rows_x, 1 - comp_y : 1 - comp_y + rows_y, :
        ]
        moved.append(jnp.roll(plane, comp_z, axis=2))
    return jnp.stack(moved)


def outlet_mean(current, kinds, onehot):
    density = jnp.sum(current, axis=0)
    is_outlet = kinds == 3
    column = jnp.sum(jnp.where(is_outlet, density, 0.0), axis=2).reshape(-1)
    col_count = jnp.sum(is_outlet.astype(jnp.float32), axis=2).reshape(-1)
    local_sums = jnp.dot(onehot, column, precision=lax.Precision.HIGHEST)
    local_counts = jnp.dot(onehot, col_count, precision=lax.Precision.HIGHEST)
    totals, counts = lax.psum((local_sums, local_counts), ("gx", "gy"))
    return totals / counts


def widen_first(post, from_lower, from_upper):
    blank = jnp.zeros_like(post[0, :1])
    planes = []
    for number in range(19):
        lower = from_lower[RISING_X.index(number)][None] if number in RISING_X else blank
        upper = from_upper[FALLING_X.index(number)][None] if number in FALLING_X else blank
        planes.append(jnp.concatenate([lower, post[number], upper], axis=0))
    return planes


def widen_second(planes, from_lower, from_upper):
    blank = jnp.zeros_like(planes[0][:, :1])
    padded = []
    for number in range(19):
        lower = from_lower[RISING_Y.index(number)][:, None] if number in RISING_Y else blank
        upper = from_upper[FALLING_Y.index(number)][:, None] if number in FALLING_Y else blank
        padded.append(jnp.concatenate([lower, planes[number], upper], axis=1))
    return jnp.stack(padded)


def body(populations, cell_kind, outlet_region):
    cells_x = populations.shape[1]
    cells_y = populations.shape[2]
    labels = jnp.arange(REGIONS, dtype=jnp.int32)
    onehot = (outlet_region.reshape(-1)[None, :] == labels[:, None]).astype(jnp.float32)
    current = populations
    means = []
    for timestep in range(STEPS):
        region_mean = outlet_mean(current, cell_kind, onehot)
        means.append(region_mean)
        col_mean = jnp.dot(region_mean, onehot, precision=lax.Precision.HIGHEST).reshape(
            cells_x, cells_y
        )[:, :, None]
        post = collide(current, cell_kind, col_mean)
        lower_x = from_behind(jnp.stack([post[number, -1] for number in RISING_X]), "gx", 1)
        upper_x = from_behind(jnp.stack([post[number, 0] for number in FALLING_X]), "gx", -1)
        planes = widen_first(post, lower_x, upper_x)
        lower_y = from_behind_2(jnp.stack([planes[number][:, -1] for number in RISING_Y]), "gy", 1)
        upper_y = from_behind_2(jnp.stack([planes[number][:, 0] for number in FALLING_Y]), "gy", -1)
        padded = widen_second(planes, lower_y, upper_y)
        current = stream(padded, cells_x, cells_y)
    return (current, jnp.stack(means))


def solution(mesh):
    in_specs = (P(None, "gx", "gy", None), P("gx", "gy", None), P("gx", "gy"))
    out_specs = (P(None, "gx", "gy", None), P())
    return jax.shard_map(body, mesh=mesh, in_specs=in_specs, out_specs=out_specs, check_vma=False)
```

profile of v0, /device:TPU:1, one launch (start us, length us, event | category | flops | bytes accessed | tf_op | source)
XLA Modules:
  0.0 127.7 jit_solution(15017054482665278097)
XLA Ops:
  0.7 0.8 constant_dynamic-update-slice_fusion.47
  1.5 1.1 reduce_sum.854
  2.6 0.1 constant_dynamic-update-slice_fusion.66
  2.7 0.7 copy-done.1
  3.4 0.1 convert_reduce_fusion
  4.1 0.6 copy-done.2
  4.8 0.1 convolution_bitcast_fusion.3
  4.9 0.2 convolution_bitcast_fusion.4
  5.1 40.5 %all-reduce = (f32[64]{0:T(128)S(1)}, f32[64]{0:T(128)S(1)}) all-reduce(f32[64]{0:T(128)S(1)} %convolution_bitcast_fusion.4, f32[64]{0:T(128)S(1)} %convolution_bitcast_fusion.3), channel_id=1, replica_groups=mesh['gx'=4,'gy'=8] {'gx','gy'}, use_global_device_ids=true, to_apply=%region_2.3 | all-reduce | flops 128 | bytes 1024 | tf_op jit(solution)/shard_map/psum | solution.py:109
  45.6 0.1 broadcast_multiply_fusion.2
  47.8 0.3 select_select_fusion.1
  48.2 5.3 %collective-permute-start = (f32[5,8,128]{2,1,0:T(8,128)S(1)}, f32[5,8,128]{2,1,0:T(8,128)S(1)}, u32[]{:S(2)}, u32[]{:S(2)}) collective-permute-start(f32[5,8,128]{2,1,0:T(8,128)S(1)} %get-tuple-element.153), channel_id=1, source_target_pairs={{0,8},{8,16},{16,24},{1,9},{9,17},{17,25},{2,10},{10,18},{18,26},{... | collective-permute-start | bytes 61448 | tf_op jit(solution)/shard_map/ppermute | solution.py:42
  53.5 1.9 %collective-permute-start.1 = (f32[5,8,128]{2,1,0:T(8,128)S(1)}, f32[5,8,128]{2,1,0:T(8,128)S(1)}, u32[]{:S(2)}, u32[]{:S(2)}) collective-permute-start(f32[5,8,128]{2,1,0:T(8,128)S(1)} %get-tuple-element.154), channel_id=1, source_target_pairs={{8,0},{16,8},{24,16},{9,1},{17,9},{25,17},{10,2},{18,10},{26,18},{... | collective-permute-start | bytes 61448 | tf_op jit(solution)/shard_map/ppermute | solution.py:42
  55.5 3.1 %collective-permute-done.1 = f32[5,8,128]{2,1,0:T(8,128)S(1)} collective-permute-done((f32[5,8,128]{2,1,0:T(8,128)S(1)}, f32[5,8,128]{2,1,0:T(8,128)S(1)}, u32[]{:S(2)}, u32[]{:S(2)}) %collective-permute-start.1) | collective-permute-done | bytes 20512 | tf_op jit(solution)/shard_map/ppermute | solution.py:42
  58.7 0.3 collective-permute-start.2
  59.2 4.0 %collective-permute-start.3 = (f32[5,10,128]{2,0,1:T(8,128)S(1)}, f32[5,10,128]{2,0,1:T(8,128)S(1)}, u32[]{:S(2)}, u32[]{:S(2)}) collective-permute-start(f32[5,10,128]{2,0,1:T(8,128)S(1)} %stack.147), channel_id=1, source_target_pairs={{0,7},{1,0},{2,1},{3,2},{4,3},{5,4},{6,5},{7,6},{8,15},{9,8},{10,9... | collective-permute-start | bytes 76808 | tf_op jit(solution)/shard_map/ppermute | solution.py:48
  63.2 1.1 collective-permute-done.2
  65.7 0.3 constant_dynamic-update-slice_fusion.152
  66.8 0.1 fusion.168
  67.0 0.1 convolution_bitcast_fusion.1
  67.2 38.7 %psum.26 = f32[64]{0:T(128)S(1)} all-reduce(f32[64]{0:T(128)S(1)} %convolution_bitcast_fusion.1), channel_id=1, replica_groups=mesh['gx'=4,'gy'=8] {'gx','gy'}, use_global_device_ids=true, to_apply=%region_6.7 | all-reduce | flops 64 | bytes 512 | tf_op jit(solution)/shard_map/psum | solution.py:109
  105.9 0.1 broadcast_multiply_fusion.1
  106.3 0.1 constant_dynamic-update-slice_fusion.94
  107.7 0.3 select_select_fusion
  108.2 5.3 %collective-permute-start.4 = (f32[5,8,128]{2,1,0:T(8,128)S(1)}, f32[5,8,128]{2,1,0:T(8,128)S(1)}, u32[]{:S(2)}, u32[]{:S(2)}) collective-permute-start(f32[5,8,128]{2,1,0:T(8,128)S(1)} %get-tuple-element.125), channel_id=1, source_target_pairs={{0,8},{8,16},{16,24},{1,9},{9,17},{17,25},{2,10},{10,18},{18,26},{... | collective-permute-start | bytes 61448 | tf_op jit(solution)/shard_map/ppermute | solution.py:42
  113.4 1.9 %collective-permute-start.5 = (f32[5,8,128]{2,1,0:T(8,128)S(1)}, f32[5,8,128]{2,1,0:T(8,128)S(1)}, u32[]{:S(2)}, u32[]{:S(2)}) collective-permute-start(f32[5,8,128]{2,1,0:T(8,128)S(1)} %get-tuple-element.124), channel_id=1, source_target_pairs={{8,0},{16,8},{24,16},{9,1},{17,9},{25,17},{10,2},{18,10},{26,18},{... | collective-permute-start | bytes 61448 | tf_op jit(solution)/shard_map/ppermute | solution.py:42
  115.4 0.6 pad_maximum_fusion.164
  116.0 2.6 %collective-permute-done.5 = f32[5,8,128]{2,1,0:T(8,128)S(1)} collective-permute-done((f32[5,8,128]{2,1,0:T(8,128)S(1)}, f32[5,8,128]{2,1,0:T(8,128)S(1)}, u32[]{:S(2)}, u32[]{:S(2)}) %collective-permute-start.5) | collective-permute-done | bytes 20512 | tf_op jit(solution)/shard_map/ppermute | solution.py:42
  118.7 0.8 collective-permute-start.7
  119.5 0.7 collective-permute-start.6
  120.7 4.5 %collective-permute-done.6 = f32[5,10,128]{2,0,1:T(8,128)S(1)} collective-permute-done((f32[5,10,128]{2,0,1:T(8,128)S(1)}, f32[5,10,128]{2,0,1:T(8,128)S(1)}, u32[]{:S(2)}, u32[]{:S(2)}) %collective-permute-start.6) | collective-permute-done | bytes 25632 | tf_op jit(solution)/shard_map/ppermute | solution.py:48
  126.9 0.8 copy-done.3
  (263 shorter events, 8.4 us)
Async XLA Ops:
  0.6 2.0 %copy-start = (f32[19,8,8,128]{3,2,1,0:T(8,128)S(1)}, f32[19,8,8,128]{3,2,1,0:T(8,128)}, u32[]{:S(2)}) copy-start(f32[19,8,8,128]{3,2,1,0:T(8,128)} %param.3) | copy-start | bytes 1867780
  2.6 0.8 copy-start.1
  4.0 0.7 copy-start.2
  48.2 10.4 %collective-permute-start = (f32[5,8,128]{2,1,0:T(8,128)S(1)}, f32[5,8,128]{2,1,0:T(8,128)S(1)}, u32[]{:S(2)}, u32[]{:S(2)}) collective-permute-start(f32[5,8,128]{2,1,0:T(8,128)S(1)} %get-tuple-element.153), channel_id=1, source_target_pairs={{0,8},{8,16},{16,24},{1,9},{9,17},{17,25},{2,10},{10,18},{18,26},{... | collective-permute-start | bytes 61448 | tf_op jit(solution)/shard_map/ppermute | solution.py:42
  53.5 5.1 %collective-permute-start.1 = (f32[5,8,128]{2,1,0:T(8,128)S(1)}, f32[5,8,128]{2,1,0:T(8,128)S(1)}, u32[]{:S(2)}, u32[]{:S(2)}) collective-permute-start(f32[5,8,128]{2,1,0:T(8,128)S(1)} %get-tuple-element.154), channel_id=1, source_target_pairs={{8,0},{16,8},{24,16},{9,1},{17,9},{25,17},{10,2},{18,10},{26,18},{... | collective-permute-start | bytes 61448 | tf_op jit(solution)/shard_map/ppermute | solution.py:42
  58.7 5.6 %collective-permute-start.2 = (f32[5,10,128]{2,0,1:T(8,128)S(1)}, f32[5,10,128]{2,0,1:T(8,128)S(1)}, u32[]{:S(2)}, u32[]{:S(2)}) collective-permute-start(f32[5,10,128]{2,0,1:T(8,128)S(1)} %stack.145), channel_id=1, source_target_pairs={{0,1},{1,2},{2,3},{3,4},{4,5},{5,6},{6,7},{7,0},{8,9},{9,10},{10,1... | collective-permute-start | bytes 76808 | tf_op jit(solution)/shard_map/ppermute | solution.py:48
  59.2 5.2 %collective-permute-start.3 = (f32[5,10,128]{2,0,1:T(8,128)S(1)}, f32[5,10,128]{2,0,1:T(8,128)S(1)}, u32[]{:S(2)}, u32[]{:S(2)}) collective-permute-start(f32[5,10,128]{2,0,1:T(8,128)S(1)} %stack.147), channel_id=1, source_target_pairs={{0,7},{1,0},{2,1},{3,2},{4,3},{5,4},{6,5},{7,6},{8,15},{9,8},{10,9... | collective-permute-start | bytes 76808 | tf_op jit(solution)/shard_map/ppermute | solution.py:48
  108.2 7.8 %collective-permute-start.4 = (f32[5,8,128]{2,1,0:T(8,128)S(1)}, f32[5,8,128]{2,1,0:T(8,128)S(1)}, u32[]{:S(2)}, u32[]{:S(2)}) collective-permute-start(f32[5,8,128]{2,1,0:T(8,128)S(1)} %get-tuple-element.125), channel_id=1, source_target_pairs={{0,8},{8,16},{16,24},{1,9},{9,17},{17,25},{2,10},{10,18},{18,26},{... | collective-permute-start | bytes 61448 | tf_op jit(solution)/shard_map/ppermute | solution.py:42
  113.4 5.1 %collective-permute-start.5 = (f32[5,8,128]{2,1,0:T(8,128)S(1)}, f32[5,8,128]{2,1,0:T(8,128)S(1)}, u32[]{:S(2)}, u32[]{:S(2)}) collective-permute-start(f32[5,8,128]{2,1,0:T(8,128)S(1)} %get-tuple-element.124), channel_id=1, source_target_pairs={{8,0},{16,8},{24,16},{9,1},{17,9},{25,17},{10,2},{18,10},{26,18},{... | collective-permute-start | bytes 61448 | tf_op jit(solution)/shard_map/ppermute | solution.py:42
  118.7 6.9 %collective-permute-start.7 = (f32[5,10,128]{2,0,1:T(8,128)S(1)}, f32[5,10,128]{2,0,1:T(8,128)S(1)}, u32[]{:S(2)}, u32[]{:S(2)}) collective-permute-start(f32[5,10,128]{2,0,1:T(8,128)S(1)} %stack.347), channel_id=1, source_target_pairs={{0,7},{1,0},{2,1},{3,2},{4,3},{5,4},{6,5},{7,6},{8,15},{9,8},{10,9... | collective-permute-start | bytes 76808 | tf_op jit(solution)/shard_map/ppermute | solution.py:48
  119.5 5.6 %collective-permute-start.6 = (f32[5,10,128]{2,0,1:T(8,128)S(1)}, f32[5,10,128]{2,0,1:T(8,128)S(1)}, u32[]{:S(2)}, u32[]{:S(2)}) collective-permute-start(f32[5,10,128]{2,0,1:T(8,128)S(1)} %stack.172), channel_id=1, source_target_pairs={{0,1},{1,2},{2,3},{3,4},{4,5},{5,6},{6,7},{7,0},{8,9},{9,10},{10,1... | collective-permute-start | bytes 76808 | tf_op jit(solution)/shard_map/ppermute | solution.py:48
  126.9 0.8 copy-start.3
where the time goes:
time: 128 us
  blocking collectives  79.2 us (62%)
  starting transfers between devices  20.2 us (16%)
  waiting for transfers between devices  11.3 us (9%)
  other arithmetic  8.05 us (6%)
  local copies, waits for them, and re-layouts  6.31 us (5%)
  between operations  2.01 us (2%)
    psum x2, blocking collectives, outlet_mean(): totals, counts = lax.psum((local_sums, local_counts), ('gx', 'gy'))  79.2 us
    ppermute x4, starting transfers between devices, from_behind(): return lax.ppermute(block, axis, route)  14.4 us
    ppermute x4, starting transfers between devices, from_behind_2(): return lax.ppermute(value, axis, pairs)  5.84 us
    ppermute x4, waiting for transfers between devices, from_behind(): return lax.ppermute(block, axis, route)  5.67 us
    ppermute x4, waiting for transfers between devices, from_behind_2(): return lax.ppermute(value, axis, pairs)  5.62 us
    unnamed x80, other arithmetic  4.53 us
    unnamed x79, local copies, waits for them, and re-layouts  3.4 us
  transfers between devices with their start and end apart: 8, of which 4 were waited for; matrix products, arithmetic and copies ran while one was open for 1% of the time, Pallas kernels for 0%

commit v1 on v0

--- a/solution.py
+++ b/solution.py
@@ -1,3 +1,4 @@
+import functools
 import jax
 import jax.numpy as jnp
 from jax import lax
@@ -34,6 +35,13 @@
 FALLING_X = (2, 8, 10, 12, 14)
 RISING_Y = (3, 7, 10, 15, 17)
 FALLING_Y = (4, 8, 9, 16, 18)
+
+
+def launch_squares(mine_x, which_axis, lane_axis):
+    return lax.psum(lax.psum(mine_x, which_axis), lane_axis)
+
+
+track_numbers = functools.partial(launch_squares, which_axis="gx", lane_axis="gy")
 
 
 def from_behind(block, axis, distance):
@@ -106,7 +114,7 @@
     col_count = jnp.sum(is_outlet.astype(jnp.float32), axis=2).reshape(-1)
     local_sums = jnp.dot(onehot, column, precision=lax.Precision.HIGHEST)
     local_counts = jnp.dot(onehot, col_count, precision=lax.Precision.HIGHEST)
-    totals, counts = lax.psum((local_sums, local_counts), ("gx", "gy"))
+    totals, counts = track_numbers((local_sums, local_counts))
     return totals / counts
 
 

time: 128 us -> 101 us (0.79)
  blocking collectives: 79.2 us -> 47.5 us
  starting transfers between devices: 20.2 us -> 25.1 us
    psum x2 -> x4, blocking collectives: 79.2 us -> 47.5 us  [launch_squares(): return lax.psum(lax.psum(mine_x, which_axis), lane_axis)]
    ppermute x4, starting transfers between devices: 14.4 us -> 19.3 us  [from_behind(): return lax.ppermute(block, axis, route)]
  transfers between devices with their start and end apart: 8 -> 8, of which waited for: 4 -> 4; matrix products, arithmetic and copies ran while one was open for 1% -> 2% of each run, Pallas kernels for 0% -> 0%
where the time goes in v1:
time: 101 us; the launch traced here: 100 us
  blocking collectives  47.5 us (47%)
  starting transfers between devices  25.1 us (25%)
  waiting for transfers between devices  10.5 us (10%)
  other arithmetic  8.06 us (8%)
  local copies, waits for them, and re-layouts  6.31 us (6%)
  between operations  2.03 us (2%)
    psum x4, blocking collectives, launch_squares(): return lax.psum(lax.psum(mine_x, which_axis), lane_axis)  47.5 us
    ppermute x4, starting transfers between devices, from_behind(): return lax.ppermute(block, axis, route)  19.3 us
    ppermute x4, starting transfers between devices, from_behind_2(): return lax.ppermute(value, axis, pairs)  5.81 us
    ppermute x4, waiting for transfers between devices, from_behind(): return lax.ppermute(block, axis, route)  5.67 us
    ppermute x4, waiting for transfers between devices, from_behind_2(): return lax.ppermute(value, axis, pairs)  4.86 us
    unnamed x80, other arithmetic  4.53 us
    unnamed x79, local copies, waits for them, and re-layouts  3.41 us
  transfers between devices with their start and end apart: 8, of which 4 were waited for; matrix products, arithmetic and copies ran while one was open for 2% of the time, Pallas kernels for 0%

profile of v1, /device:TPU:1, one launch (start us, length us, event | category | flops | bytes accessed | tf_op | source)
XLA Modules:
  0.0 100.2 jit_solution(17245517884360447215)
XLA Ops:
  0.7 0.8 constant_dynamic-update-slice_fusion.47
  1.5 1.1 %reduce_sum.854 = f32[8,8,128]{2,1,0:T(8,128)S(1)} reduce(f32[19,8,8,128]{3,2,1,0:T(8,128)} %param.3, f32[]{:T(128)} %constant.20.clone.1), dimensions={0}, to_apply=%region_0.0 | reduce | flops 147456 | bytes 655364 | tf_op jit(solution)/shard_map/reduce_sum | solution.py:111
  2.6 0.1 constant_dynamic-update-slice_fusion.66
  2.7 0.7 copy-done.1
  3.4 0.1 convert_reduce_fusion
  4.1 0.6 copy-done.2
  4.8 0.1 convolution_bitcast_fusion.3
  4.9 0.2 convolution_bitcast_fusion.4
  5.1 6.4 %all-reduce.1 = (f32[64]{0:T(128)S(1)}, f32[64]{0:T(128)S(1)}) all-reduce(f32[64]{0:T(128)S(1)} %convolution_bitcast_fusion.4, f32[64]{0:T(128)S(1)} %convolution_bitcast_fusion.3), channel_id=1, replica_groups=mesh['gx'=4,'gy'=8] {'gx'}, use_global_device_ids=true, to_apply=%region_2.3 | all-reduce | flops 128 | bytes 1024 | tf_op jit(solution)/shard_map/psum | solution.py:41
  11.5 18.0 %all-reduce = (f32[64]{0:T(128)S(1)}, f32[64]{0:T(128)S(1)}) all-reduce(f32[64]{0:T(128)S(1)} %get-tuple-element.8, f32[64]{0:T(128)S(1)} %get-tuple-element.9), channel_id=1, replica_groups=mesh['gx'=4,'gy'=8] {'gy'}, use_global_device_ids=true, to_apply=%region_3.4 | all-reduce | flops 128 | bytes 1024 | tf_op jit(solution)/shard_map/psum | solution.py:41
  29.5 0.1 broadcast_multiply_fusion.2
  31.7 0.3 select_select_fusion.1
  32.1 7.6 %collective-permute-start = (f32[5,8,128]{2,1,0:T(8,128)S(1)}, f32[5,8,128]{2,1,0:T(8,128)S(1)}, u32[]{:S(2)}, u32[]{:S(2)}) collective-permute-start(f32[5,8,128]{2,1,0:T(8,128)S(1)} %get-tuple-element.155), channel_id=1, source_target_pairs={{0,8},{8,16},{16,24},{1,9},{9,17},{17,25},{2,10},{10,18},{18,26},{... | collective-permute-start | bytes 61448 | tf_op jit(solution)/shard_map/ppermute | solution.py:50
  39.8 1.9 %collective-permute-start.1 = (f32[5,8,128]{2,1,0:T(8,128)S(1)}, f32[5,8,128]{2,1,0:T(8,128)S(1)}, u32[]{:S(2)}, u32[]{:S(2)}) collective-permute-start(f32[5,8,128]{2,1,0:T(8,128)S(1)} %get-tuple-element.156), channel_id=1, source_target_pairs={{8,0},{16,8},{24,16},{9,1},{17,9},{25,17},{10,2},{18,10},{26,18},{... | collective-permute-start | bytes 61448 | tf_op jit(solution)/shard_map/ppermute | solution.py:50
  41.8 3.1 %collective-permute-done.1 = f32[5,8,128]{2,1,0:T(8,128)S(1)} collective-permute-done((f32[5,8,128]{2,1,0:T(8,128)S(1)}, f32[5,8,128]{2,1,0:T(8,128)S(1)}, u32[]{:S(2)}, u32[]{:S(2)}) %collective-permute-start.1) | collective-permute-done | bytes 20512 | tf_op jit(solution)/shard_map/ppermute | solution.py:50
  45.3 4.2 %collective-permute-start.3 = (f32[5,10,128]{2,0,1:T(8,128)S(1)}, f32[5,10,128]{2,0,1:T(8,128)S(1)}, u32[]{:S(2)}, u32[]{:S(2)}) collective-permute-start(f32[5,10,128]{2,0,1:T(8,128)S(1)} %stack.147), channel_id=1, source_target_pairs={{0,7},{1,0},{2,1},{3,2},{4,3},{5,4},{6,5},{7,6},{8,15},{9,8},{10,9... | collective-permute-start | bytes 76808 | tf_op jit(solution)/shard_map/ppermute | solution.py:56
  49.5 1.1 %collective-permute-done.2 = f32[5,10,128]{2,0,1:T(8,128)S(1)} collective-permute-done((f32[5,10,128]{2,0,1:T(8,128)S(1)}, f32[5,10,128]{2,0,1:T(8,128)S(1)}, u32[]{:S(2)}, u32[]{:S(2)}) %collective-permute-start.2) | collective-permute-done | bytes 25632 | tf_op jit(solution)/shard_map/ppermute | solution.py:56
  52.0 0.3 constant_dynamic-update-slice_fusion.152
  53.1 0.1 fusion.168
  53.3 0.1 convolution_bitcast_fusion.1
  53.5 5.1 %psum.52 = f32[64]{0:T(128)S(1)} all-reduce(f32[64]{0:T(128)S(1)} %convolution_bitcast_fusion.1), channel_id=1, replica_groups=mesh['gx'=4,'gy'=8] {'gx'}, use_global_device_ids=true, to_apply=%region_8.9 | all-reduce | flops 64 | bytes 512 | tf_op jit(solution)/shard_map/psum | solution.py:41
  58.6 18.0 %psum.53 = f32[64]{0:T(128)S(1)} all-reduce(f32[64]{0:T(128)S(1)} %psum.52), channel_id=1, replica_groups=mesh['gx'=4,'gy'=8] {'gy'}, use_global_device_ids=true, to_apply=%region_9.10 | all-reduce | flops 64 | bytes 512 | tf_op jit(solution)/shard_map/psum | solution.py:41
  76.6 0.1 broadcast_multiply_fusion.1
  77.0 0.1 constant_dynamic-update-slice_fusion.94
  78.4 0.3 select_select_fusion
  78.9 7.8 %collective-permute-start.4 = (f32[5,8,128]{2,1,0:T(8,128)S(1)}, f32[5,8,128]{2,1,0:T(8,128)S(1)}, u32[]{:S(2)}, u32[]{:S(2)}) collective-permute-start(f32[5,8,128]{2,1,0:T(8,128)S(1)} %get-tuple-element.127), channel_id=1, source_target_pairs={{0,8},{8,16},{16,24},{1,9},{9,17},{17,25},{2,10},{10,18},{18,26},{... | collective-permute-start | bytes 61448 | tf_op jit(solution)/shard_map/ppermute | solution.py:50
  86.7 1.9 %collective-permute-start.5 = (f32[5,8,128]{2,1,0:T(8,128)S(1)}, f32[5,8,128]{2,1,0:T(8,128)S(1)}, u32[]{:S(2)}, u32[]{:S(2)}) collective-permute-start(f32[5,8,128]{2,1,0:T(8,128)S(1)} %get-tuple-element.126), channel_id=1, source_target_pairs={{8,0},{16,8},{24,16},{9,1},{17,9},{25,17},{10,2},{18,10},{26,18},{... | collective-permute-start | bytes 61448 | tf_op jit(solution)/shard_map/ppermute | solution.py:50
  88.7 0.6 pad_maximum_fusion.164
  89.3 2.6 %collective-permute-done.5 = f32[5,8,128]{2,1,0:T(8,128)S(1)} collective-permute-done((f32[5,8,128]{2,1,0:T(8,128)S(1)}, f32[5,8,128]{2,1,0:T(8,128)S(1)}, u32[]{:S(2)}, u32[]{:S(2)}) %collective-permute-start.5) | collective-permute-done | bytes 20512 | tf_op jit(solution)/shard_map/ppermute | solution.py:50
  92.1 1.5 %collective-permute-start.6 = (f32[5,10,128]{2,0,1:T(8,128)S(1)}, f32[5,10,128]{2,0,1:T(8,128)S(1)}, u32[]{:S(2)}, u32[]{:S(2)}) collective-permute-start(f32[5,10,128]{2,0,1:T(8,128)S(1)} %stack.172), channel_id=1, source_target_pairs={{0,1},{1,2},{2,3},{3,4},{4,5},{5,6},{6,7},{7,0},{8,9},{9,10},{10,1... | collective-permute-start | bytes 76808 | tf_op jit(solution)/shard_map/ppermute | solution.py:56
  93.9 3.7 %collective-permute-done.6 = f32[5,10,128]{2,0,1:T(8,128)S(1)} collective-permute-done((f32[5,10,128]{2,0,1:T(8,128)S(1)}, f32[5,10,128]{2,0,1:T(8,128)S(1)}, u32[]{:S(2)}, u32[]{:S(2)}) %collective-permute-start.6) | collective-permute-done | bytes 25632 | tf_op jit(solution)/shard_map/ppermute | solution.py:56
  99.4 0.8 copy-done.3
  (265 shorter events, 8.6 us)
Async XLA Ops:
  0.6 2.0 %copy-start = (f32[19,8,8,128]{3,2,1,0:T(8,128)S(1)}, f32[19,8,8,128]{3,2,1,0:T(8,128)}, u32[]{:S(2)}) copy-start(f32[19,8,8,128]{3,2,1,0:T(8,128)} %param.3) | copy-start | bytes 1867780
  2.6 0.8 copy-start.1
  4.0 0.7 copy-start.2
  32.1 12.8 %collective-permute-start = (f32[5,8,128]{2,1,0:T(8,128)S(1)}, f32[5,8,128]{2,1,0:T(8,128)S(1)}, u32[]{:S(2)}, u32[]{:S(2)}) collective-permute-start(f32[5,8,128]{2,1,0:T(8,128)S(1)} %get-tuple-element.155), channel_id=1, source_target_pairs={{0,8},{8,16},{16,24},{1,9},{9,17},{17,25},{2,10},{10,18},{18,26},{... | collective-permute-start | bytes 61448 | tf_op jit(solution)/shard_map/ppermute | solution.py:50
  39.8 5.1 %collective-permute-start.1 = (f32[5,8,128]{2,1,0:T(8,128)S(1)}, f32[5,8,128]{2,1,0:T(8,128)S(1)}, u32[]{:S(2)}, u32[]{:S(2)}) collective-permute-start(f32[5,8,128]{2,1,0:T(8,128)S(1)} %get-tuple-element.156), channel_id=1, source_target_pairs={{8,0},{16,8},{24,16},{9,1},{17,9},{25,17},{10,2},{18,10},{26,18},{... | collective-permute-start | bytes 61448 | tf_op jit(solution)/shard_map/ppermute | solution.py:50
  45.0 5.6 %collective-permute-start.2 = (f32[5,10,128]{2,0,1:T(8,128)S(1)}, f32[5,10,128]{2,0,1:T(8,128)S(1)}, u32[]{:S(2)}, u32[]{:S(2)}) collective-permute-start(f32[5,10,128]{2,0,1:T(8,128)S(1)} %stack.145), channel_id=1, source_target_pairs={{0,1},{1,2},{2,3},{3,4},{4,5},{5,6},{6,7},{7,0},{8,9},{9,10},{10,1... | collective-permute-start | bytes 76808 | tf_op jit(solution)/shard_map/ppermute | solution.py:56
  45.3 5.5 %collective-permute-start.3 = (f32[5,10,128]{2,0,1:T(8,128)S(1)}, f32[5,10,128]{2,0,1:T(8,128)S(1)}, u32[]{:S(2)}, u32[]{:S(2)}) collective-permute-start(f32[5,10,128]{2,0,1:T(8,128)S(1)} %stack.147), channel_id=1, source_target_pairs={{0,7},{1,0},{2,1},{3,2},{4,3},{5,4},{6,5},{7,6},{8,15},{9,8},{10,9... | collective-permute-start | bytes 76808 | tf_op jit(solution)/shard_map/ppermute | solution.py:56
  78.9 10.3 %collective-permute-start.4 = (f32[5,8,128]{2,1,0:T(8,128)S(1)}, f32[5,8,128]{2,1,0:T(8,128)S(1)}, u32[]{:S(2)}, u32[]{:S(2)}) collective-permute-start(f32[5,8,128]{2,1,0:T(8,128)S(1)} %get-tuple-element.127), channel_id=1, source_target_pairs={{0,8},{8,16},{16,24},{1,9},{9,17},{17,25},{2,10},{10,18},{18,26},{... | collective-permute-start | bytes 61448 | tf_op jit(solution)/shard_map/ppermute | solution.py:50
  86.7 5.1 %collective-permute-start.5 = (f32[5,8,128]{2,1,0:T(8,128)S(1)}, f32[5,8,128]{2,1,0:T(8,128)S(1)}, u32[]{:S(2)}, u32[]{:S(2)}) collective-permute-start(f32[5,8,128]{2,1,0:T(8,128)S(1)} %get-tuple-element.126), channel_id=1, source_target_pairs={{8,0},{16,8},{24,16},{9,1},{17,9},{25,17},{10,2},{18,10},{26,18},{... | collective-permute-start | bytes 61448 | tf_op jit(solution)/shard_map/ppermute | solution.py:50
  91.9 6.2 %collective-permute-start.7 = (f32[5,10,128]{2,0,1:T(8,128)S(1)}, f32[5,10,128]{2,0,1:T(8,128)S(1)}, u32[]{:S(2)}, u32[]{:S(2)}) collective-permute-start(f32[5,10,128]{2,0,1:T(8,128)S(1)} %stack.347), channel_id=1, source_target_pairs={{0,7},{1,0},{2,1},{3,2},{4,3},{5,4},{6,5},{7,6},{8,15},{9,8},{10,9... | collective-permute-start | bytes 76808 | tf_op jit(solution)/shard_map/ppermute | solution.py:56
  92.1 5.6 %collective-permute-start.6 = (f32[5,10,128]{2,0,1:T(8,128)S(1)}, f32[5,10,128]{2,0,1:T(8,128)S(1)}, u32[]{:S(2)}, u32[]{:S(2)}) collective-permute-start(f32[5,10,128]{2,0,1:T(8,128)S(1)} %stack.172), channel_id=1, source_target_pairs={{0,1},{1,2},{2,3},{3,4},{4,5},{5,6},{6,7},{7,0},{8,9},{9,10},{10,1... | collective-permute-start | bytes 76808 | tf_op jit(solution)/shard_map/ppermute | solution.py:56
  99.4 0.8 copy-start.3
